TPU v7x, 128 devices: a whole 4x4x4 slice. The times are simulated.
128 devices in a mesh: tier: 16 (over y, z), mat: 8 (over x, core).
Axes of the slice: x: 4, y: 4, z: 4, core: 2. Of those that a mesh axis runs over, the one named last changes fastest.
Arguments:
- costate: bfloat16 [512, 2, 256, 256], P(('tier', 'mat')), may hold values from -6 to 6
- hamiltonian: bfloat16 [256, 256], replicated, may hold values from -0.375 to 0.375
- couplers: bfloat16 [3, 256, 256], replicated, may hold values from -0.375 to 0.375
- damping: float32 [12], replicated, may hold values from 0.05 to 0.5
- coupling: float32 [2, 12], replicated, may hold values from -0.9 to 0.9
- levels: int32 [512, 12], P(('tier', 'mat')), may hold values from 0 to 3
- neighbour_slot: int32 [512, 24], P(('tier', 'mat')), may hold values from 0 to 31
- neighbour_mode: int32 [512, 24], P(('tier', 'mat')), may hold values from 0 to 11
- neighbour_flag: int32 [512, 24], P(('tier', 'mat')), may hold values from -1 to 1
- send_index: int32 [128, 32], P(('tier', 'mat')), may hold values from 0 to 3
Outputs:
- increment: float32 [512, 2, 256, 256], P(('tier', 'mat'))
- bath_gradient: float32 [12], replicated
All inputs are finite; a program needn't handle non-finite values.
Results may differ from a plain program's by a relative error of at most 0.0053.
Values may be sent and summed in bfloat16 or wider, within the bound.
No kernel may reach another device: no remote copies, remote signals or barrier semaphores. Data moves between devices by JAX's collectives and lax.ppermute only.
A program may use at most 128 MiB of HBM per device.

v0:
```python
import jax
import jax.numpy as jnp
from jax import lax
from jax.sharding import Mesh
from jax.sharding import PartitionSpec as P

MODES = 12
TIER = ("tier_0", "tier_1")
TIER_MAT = ("tier_0", "tier_1", "mat_0", "mat_1")


def cut_along(value, dim, devices):
    before, after = (value.shape[:dim], value.shape[dim + 1 :])
    return jnp.moveaxis(value.reshape(*before, devices, -1, *after), dim, 0)


def cut_rows(length, count):
    unit = 8 if length >= 8 * count else 1
    return [length // unit * k // count * unit for k in range(1, count)]


def laid_out(blocks, dim):
    blocks = jnp.moveaxis(blocks, 0, dim)
    shape = blocks.shape
    return blocks.reshape(*shape[:dim], shape[dim] * shape[dim + 1], *shape[dim + 2 :])


def several_exchanges(value, axis, pieces, split_dim, concat_dim):
    blocks = cut_along(value, split_dim, lax.axis_size(axis))
    cut = max(range(1, max(2, blocks.ndim - 1)), key=lambda d: blocks.shape[d])
    done = []
    for share in jnp.split(blocks, cut_rows(blocks.shape[cut], pieces), axis=cut):
        if share.size:
            done.append(lax.all_to_all(share, axis, split_axis=0, concat_axis=0, tiled=True))
    return laid_out(jnp.concatenate(done, axis=cut), concat_dim)


def over_axes(value, axes):
    for axis in axes:
        value = lax.psum(value, axis)
    return value


def symmetric(weight):
    square = weight.astype(jnp.float32)
    return ((square + jnp.swapaxes(square, -1, -2)) * 0.5).astype(jnp.bfloat16)


def receive(outgoing):
    return several_exchanges(outgoing, TIER, 2, 0, 0)


def per_device(
    costate,
    hamiltonian,
    couplers,
    damping,
    coupling,
    levels,
    neighbour_slot,
    neighbour_mode,
    neighbour_flag,
    send_index,
):
    high = lax.Precision.HIGHEST
    operators = jnp.concatenate([symmetric(hamiltonian)[None], symmetric(couplers)], 0)
    hamilton = operators[0]
    coupled = operators[1:]
    width = costate.shape[3]
    slot_count = send_index.shape[1]
    live = (neighbour_flag >= 0).astype(jnp.float32)
    mode_onehot = (neighbour_mode[:, :, None] == jnp.arange(MODES)[None, None, :]).astype(
        jnp.float32
    )
    level_here = jnp.einsum("nek,nk->ne", mode_onehot, levels.astype(jnp.float32), precision=high)
    weight = jnp.sqrt(1.0 + level_here) * live
    coup_real = jnp.einsum("nek,k->ne", mode_onehot, coupling[0], precision=high) * weight
    coup_imag = jnp.einsum("nek,k->ne", mode_onehot, coupling[1], precision=high) * weight
    right_imag = jnp.where(neighbour_flag == 1, coup_imag, -coup_imag)
    op_onehot = (neighbour_mode[:, :, None] % 3 == jnp.arange(3)[None, None, :]).astype(jnp.float32)
    slot_onehot = (neighbour_slot[:, :, None] == jnp.arange(slot_count)[None, None, :]).astype(
        jnp.float32
    )

    def spread(values):
        return jnp.einsum("ne,neq,nes->nqs", values, op_onehot, slot_onehot, precision=high)

    left_real = spread(coup_real)
    left_imag = spread(coup_imag)
    right_imagc = spread(right_imag)
    correlation_weight = (
        jnp.einsum("ne,nek,nes->nks", weight, mode_onehot, slot_onehot, precision=high) / width
    )
    decay = jnp.dot(levels.astype(jnp.float32), damping, precision=high)

    def combine(received_f, creal, cimag):
        sreal = jnp.einsum("nqs,sij->nqij", creal, received_f[:, 0], precision=high) - jnp.einsum(
            "nqs,sij->nqij", cimag, received_f[:, 1], precision=high
        )
        simag = jnp.einsum("nqs,sij->nqij", creal, received_f[:, 1], precision=high) + jnp.einsum(
            "nqs,sij->nqij", cimag, received_f[:, 0], precision=high
        )
        return jnp.stack([sreal, simag], 2).astype(jnp.bfloat16)

    def commutator(rotated):
        left = jnp.einsum("ij,npjk->npik", hamilton, rotated, preferred_element_type=jnp.float32)
        right = jnp.einsum("npij,jk->npik", rotated, hamilton, preferred_element_type=jnp.float32)
        return left - right

    def section(state):
        rotated = jnp.stack([-state[:, 1], state[:, 0]], 1)
        outgoing = state[send_index[0]]
        received = receive(outgoing)
        own_part = commutator(rotated)
        received_f = received.astype(jnp.float32)
        left_in = combine(received_f, left_real, left_imag)
        right_in = combine(received_f, left_real, right_imagc)
        left = jnp.einsum("qij,nqpjk->npik", coupled, left_in, preferred_element_type=jnp.float32)
        right = jnp.einsum("nqpij,qjk->npik", right_in, coupled, preferred_element_type=jnp.float32)
        rate = own_part + left - right - decay[:, None, None, None] * state.astype(jnp.float32)
        correlation = jnp.einsum(
            "npij,spij->ns", state, received, preferred_element_type=jnp.float32
        )
        grads = jnp.einsum("ns,nks->k", correlation, correlation_weight, precision=high)
        return (rate, grads)

    first, grad_first = section(costate)
    middle = (costate.astype(jnp.float32) + 0.125 * first).astype(jnp.bfloat16)
    second, grad_second = section(middle)

    def reduce_modes(values):
        return over_axes(values, TIER_MAT)

    bath_gradient = reduce_modes(grad_first) + reduce_modes(grad_second)
    return (0.25 * second, bath_gradient)


def solution(mesh):
    finer = Mesh(mesh.devices.reshape(4, 4, 4, 2), ("tier_0", "tier_1", "mat_0", "mat_1"))
    return jax.shard_map(
        per_device,
        mesh=finer,
        in_specs=(
            P(TIER_MAT, None, None, None),
            P(),
            P(),
            P(),
            P(),
            P(TIER_MAT, None),
            P(TIER_MAT, None),
            P(TIER_MAT, None),
            P(TIER_MAT, None),
            P(TIER_MAT, None),
        ),
        out_specs=(P(TIER_MAT, None, None, None), P()),
        check_vma=False,
    )
```

profile of v0, /device:TPU:1, one launch (start us, length us, event | category | flops | bytes accessed | tf_op | source)
XLA Modules:
  0.0 469.9 jit_solution(8393512838118684449)
XLA Ops:
  1.3 6.2 %gather_fusion = bf16[32,2,256,256]{3,2,1,0:T(8,128)(2,1)} fusion(bf16[4,2,256,256]{3,2,1,0:T(8,128)(2,1)} %param.10, s32[1024]{0:T(1024)S(1)} %pad_clamp_fusion), kind=kCustom, calls=%fused_computation | custom fusion | bytes 16777344 | tf_op jit(solution)/shard_map/gather | solution.py:112
  7.5 5.2 %fusion.126 = (bf16[16,2,2,128,256]{4,3,2,1,0:T(8,128)(2,1)S(1)}, bf16[16,2,2,128,256]{4,3,2,1,0:T(8,128)(2,1)}) fusion(bf16[16,2,2,256,256]{4,3,2,1,0:T(8,128)(2,1)} %bitcast.220), kind=kLoop, calls=%fused_computation.153 | loop fusion | bytes 16777216 | tf_op jit(solution)/shard_map/split | solution.py:32
  12.8 6.3 %copy.79 = bf16[16,2,2,128,256]{4,1,3,2,0:T(2,128)(2,1)} copy(bf16[16,2,2,128,256]{4,3,2,1,0:T(8,128)(2,1)S(1)} %get-tuple-element.15) | data formatting | bytes 8388608 | tf_op jit(solution)/shard_map/split | solution.py:32
  19.1 8.6 %all-to-all-start = ((bf16[16,2,2,128,256]{4,1,3,2,0:T(2,128)(2,1)}), bf16[16,2,2,128,256]{4,1,3,2,0:T(2,128)(2,1)}, u32[]{:S(2)}, u32[]{:S(2)}) async-start(bf16[16,2,2,128,256]{4,1,3,2,0:T(2,128)(2,1)} %copy.79), calls=%async_computation | async-start | bytes 8388608 | tf_op jit(solution)/shard_map/all_to_all | solution.py:34
  27.7 8.6 %copy.80 = bf16[16,2,2,128,256]{4,1,3,2,0:T(2,128)(2,1)} copy(bf16[16,2,2,128,256]{4,3,2,1,0:T(8,128)(2,1)} %get-tuple-element.16) | data formatting | bytes 8388608 | tf_op jit(solution)/shard_map/split | solution.py:32
  36.3 51.7 %all-to-all-done = bf16[16,2,2,128,256]{4,1,3,2,0:T(2,128)(2,1)} async-done(((bf16[16,2,2,128,256]{4,1,3,2,0:T(2,128)(2,1)}), bf16[16,2,2,128,256]{4,1,3,2,0:T(2,128)(2,1)}, u32[]{:S(2)}, u32[]{:S(2)}) %all-to-all-start) | async-done | bytes 4194336 | tf_op jit(solution)/shard_map/all_to_all | solution.py:34
  88.0 11.7 %all-to-all-start.1 = ((bf16[16,2,2,128,256]{4,1,3,2,0:T(2,128)(2,1)}), bf16[16,2,2,128,256]{4,1,3,2,0:T(2,128)(2,1)}, u32[]{:S(2)}, u32[]{:S(2)}) async-start(bf16[16,2,2,128,256]{4,1,3,2,0:T(2,128)(2,1)} %copy.80), calls=%async_computation.1 | async-start | bytes 8388608 | tf_op jit(solution)/shard_map/all_to_all | solution.py:34
  112.9 38.2 %all-to-all-done.1 = bf16[16,2,2,128,256]{4,1,3,2,0:T(2,128)(2,1)} async-done(((bf16[16,2,2,128,256]{4,1,3,2,0:T(2,128)(2,1)}), bf16[16,2,2,128,256]{4,1,3,2,0:T(2,128)(2,1)}, u32[]{:S(2)}, u32[]{:S(2)}) %all-to-all-start.1) | async-done | bytes 4194336 | tf_op jit(solution)/shard_map/all_to_all | solution.py:34
  151.1 12.4 %pad_maximum_fusion = bf16[16,2,2,256,256]{4,1,3,2,0:T(2,128)(2,1)S(1)} fusion(bf16[16,2,2,128,256]{4,1,3,2,0:T(2,128)(2,1)} %all-to-all-done.1, bf16[16,2,2,128,256]{4,1,3,2,0:T(2,128)(2,1)} %all-to-all-done), kind=kLoop, calls=%fused_computation.2 | loop fusion | flops 4194304 | bytes 16777216 | tf_op jit(solution)/shard_map/concatenate | solution.py:35
  163.5 9.9 %copy.81 = bf16[16,2,2,256,256]{4,1,0,3,2:T(2,128)(2,1)} copy(bf16[16,2,2,256,256]{4,1,3,2,0:T(2,128)(2,1)S(1)} %pad_maximum_fusion) | data formatting | bytes 16777216 | tf_op jit(solution)/shard_map/concatenate | solution.py:35
  173.4 13.1 %reshape.55 = bf16[32,2,256,256]{3,0,2,1:T(8,128)(2,1)} reshape(bf16[16,2,2,256,256]{4,1,0,3,2:T(2,128)(2,1)} %copy.81) | data formatting | bytes 16777216 | tf_op jit(solution)/shard_map/reshape | solution.py:25
  186.5 4.7 fusion.18
  191.2 4.5 fusion.16
  216.2 5.1 %gather_fusion.1 = bf16[32,2,256,256]{2,3,1,0:T(8,128)(2,1)} fusion(bf16[4,2,256,256]{2,3,1,0:T(8,128)(2,1)S(1)} %fusion.30, s32[1024]{0:T(1024)} %copy-done.27), kind=kCustom, calls=%fused_computation.1 | custom fusion | bytes 16777344 | tf_op jit(solution)/shard_map/gather | solution.py:112
  221.3 5.3 %fusion.125 = (bf16[16,2,2,128,256]{3,4,2,1,0:T(8,128)(2,1)S(1)}, bf16[16,2,2,128,256]{3,4,2,1,0:T(8,128)(2,1)}) fusion(bf16[16,2,2,256,256]{3,4,2,1,0:T(8,128)(2,1)} %bitcast.219), kind=kLoop, calls=%fused_computation.152 | loop fusion | bytes 16777216 | tf_op jit(solution)/shard_map/split | solution.py:32
  226.6 50.6 %all_to_all.20 = bf16[16,2,2,128,256]{3,4,2,1,0:T(8,128)(2,1)} all-to-all(bf16[16,2,2,128,256]{3,4,2,1,0:T(8,128)(2,1)S(1)} %get-tuple-element.13), channel_id=1, replica_groups=mesh['tier_0'=4,'tier_1'=4,'mat_0'=4,'mat_1'=2] {'tier_0','tier_1'}, dimensions={0} | all-to-all | bytes 8388608 | tf_op jit(solution)/shard_map/all_to_all | solution.py:34
  277.2 5.1 %all-to-all-start.3 = ((bf16[16,2,2,128,256]{3,4,2,1,0:T(8,128)(2,1)}), bf16[16,2,2,128,256]{3,4,2,1,0:T(8,128)(2,1)}, u32[]{:S(2)}, u32[]{:S(2)}) async-start(bf16[16,2,2,128,256]{3,4,2,1,0:T(8,128)(2,1)} %get-tuple-element.14), calls=%async_computation.3 | async-start | bytes 8388608 | tf_op jit(solution)/shard_map/all_to_all | solution.py:34
  288.7 6.3 %fusion = f32[32,4,1,1]{0,1,3,2:T(4,128)} fusion(bf16[32,2,256,256]{3,0,2,1:T(8,128)(2,1)} %reshape.55, bf16[4,2,256,256]{3,2,1,0:T(8,128)(2,1)S(1)} %copy-done.3), kind=kOutput, calls=%fused_computation.4 | convolution fusion | flops 33554432 | bytes 9437696 | tf_op jit(solution)/shard_map/npij,spij->ns/dot_general | solution.py:121
  294.9 38.2 %all-to-all-done.3 = bf16[16,2,2,128,256]{3,4,2,1,0:T(8,128)(2,1)} async-done(((bf16[16,2,2,128,256]{3,4,2,1,0:T(8,128)(2,1)}), bf16[16,2,2,128,256]{3,4,2,1,0:T(8,128)(2,1)}, u32[]{:S(2)}, u32[]{:S(2)}) %all-to-all-start.3) | async-done | bytes 4194336 | tf_op jit(solution)/shard_map/all_to_all | solution.py:34
  333.1 8.1 %pad_maximum_fusion.1 = bf16[16,2,2,256,256]{3,4,2,1,0:T(8,128)(2,1)} fusion(bf16[16,2,2,128,256]{3,4,2,1,0:T(8,128)(2,1)} %all-to-all-done.3, bf16[16,2,2,128,256]{3,4,2,1,0:T(8,128)(2,1)} %all_to_all.20), kind=kLoop, calls=%fused_computation.3 | loop fusion | flops 16777216 | bytes 16777216 | tf_op jit(solution)/shard_map/concatenate | solution.py:35
  341.2 14.8 %copy.107 = bf16[32,2,256,256]{3,0,1,2:T(8,128)(2,1)} copy(bf16[32,2,256,256]{2,3,1,0:T(8,128)(2,1)} %bitcast.217) | data formatting | bytes 16777216 | tf_op jit(solution)/shard_map/reshape | solution.py:25
  356.0 5.8 %fusion.127 = f32[4,32,1,1]{1,0,3,2:T(4,128)S(1)} fusion(bf16[4,2,256,256]{3,0,1,2:T(4,128)(2,1)S(1)} %copy-done.18, bf16[32,2,256,256]{3,0,1,2:T(8,128)(2,1)} %copy.107), kind=kOutput, calls=%fused_computation.154 | convolution fusion | flops 33554432 | bytes 9437696 | tf_op jit(solution)/shard_map/npij,spij->ns/dot_general | solution.py:121
  365.7 6.2 %psum.67 = f32[12]{0:T(128)S(1)} all-reduce(f32[12]{0:T(128)S(1)} %fusion.63), channel_id=1, replica_groups=mesh['tier_0'=4,'tier_1'=4,'mat_0'=4,'mat_1'=2] {'tier_0'}, use_global_device_ids=true, to_apply=%region_0.1 | all-reduce | flops 12 | bytes 96 | tf_op jit(solution)/shard_map/psum | solution.py:40
  371.9 7.9 %copy.167 = bf16[32,1,256,256]{3,0,2,1:T(8,128)(2,1)} copy(bf16[32,1,256,256]{2,3,1,0:T(8,128)(2,1)} %get-tuple-element.11) | data formatting | bytes 8388608
  379.8 6.2 %fusion.12 = f32[4,3,256,256]{3,0,2,1:T(4,128)} fusion(bf16[32,1,256,256]{3,0,2,1:T(8,128)(2,1)} %copy.167, f32[4,3,32,1]{2,1,0,3:T(4,128)S(1)} %copy-done.24), kind=kOutput, calls=%fused_computation.18 | convolution fusion | flops 301989888 | bytes 7341568 | tf_op jit(solution)/shard_map/nqs,sij->nqij/dot_general | solution.py:97
  386.0 7.9 %copy.168 = bf16[32,1,256,256]{3,0,2,1:T(8,128)(2,1)} copy(bf16[32,1,256,256]{2,3,1,0:T(8,128)(2,1)} %get-tuple-element.12) | data formatting | bytes 8388608
  394.0 7.1 %fusion.57 = bf16[4,3,1,256,256]{4,0,3,1,2:T(4,128)(2,1)} fusion(f32[4,3,256,256]{3,0,2,1:T(4,128)} %fusion.12, bf16[32,1,256,256]{3,0,2,1:T(8,128)(2,1)} %copy.168, f32[4,3,32,1]{2,1,0,3:T(4,128)S(1)} %convolution_bitcast_fusion), kind=kOutput, calls=%fused_computation.65 | convolution fusion | flops 303562752 | bytes 8914432 | tf_op jit(solution)/shard_map/nqs,sij->nqij/dot_general | solution.py:97
  405.2 12.8 %psum.66 = f32[12]{0:T(128)S(1)} all-reduce(f32[12]{0:T(128)S(1)} %psum.67), channel_id=1, replica_groups=mesh['tier_0'=4,'tier_1'=4,'mat_0'=4,'mat_1'=2] {'tier_1'}, use_global_device_ids=true, to_apply=%region_1.2 | all-reduce | flops 12 | bytes 96 | tf_op jit(solution)/shard_map/psum | solution.py:40
  418.1 6.2 %fusion.4 = f32[4,3,256,256]{3,0,2,1:T(4,128)} fusion(bf16[32,1,256,256]{3,0,2,1:T(8,128)(2,1)} %copy.168, f32[4,3,32,1]{2,1,0,3:T(4,128)S(1)} %copy-done.24), kind=kOutput, calls=%fused_computation.10 | convolution fusion | flops 301989888 | bytes 7341568 | tf_op jit(solution)/shard_map/nqs,sij->nqij/dot_general | solution.py:100
  424.3 8.6 %psum.65 = f32[12]{0:T(128)S(1)} all-reduce(f32[12]{0:T(128)S(1)} %psum.66), channel_id=1, replica_groups=mesh['tier_0'=4,'tier_1'=4,'mat_0'=4,'mat_1'=2] {'mat_0'}, use_global_device_ids=true, to_apply=%region_2.3 | all-reduce | flops 12 | bytes 96 | tf_op jit(solution)/shard_map/psum | solution.py:40
  432.9 7.1 %fusion.60 = bf16[4,3,1,256,256]{4,0,3,1,2:T(4,128)(2,1)} fusion(f32[4,3,256,256]{3,0,2,1:T(4,128)} %fusion.4, bf16[32,1,256,256]{3,0,2,1:T(8,128)(2,1)} %copy.167, f32[4,3,32,1]{2,1,0,3:T(4,128)S(1)} %convolution_bitcast_fusion), kind=kOutput, calls=%fused_computation.66 | convolution fusion | flops 303562752 | bytes 8914432 | tf_op jit(solution)/shard_map/nqs,sij->nqij/dot_general | solution.py:100
  444.2 10.5 %psum.64 = f32[12]{0:T(128)} all-reduce(f32[12]{0:T(128)S(1)} %psum.65), channel_id=1, replica_groups=mesh['tier_0'=4,'tier_1'=4,'mat_0'=4,'mat_1'=2] {'mat_1'}, use_global_device_ids=true, to_apply=%region_3.4 | all-reduce | flops 12 | bytes 96 | tf_op jit(solution)/shard_map/psum | solution.py:40
  (110 shorter events, 67.5 us)
Async XLA Ops:
  0.6 102.4 %copy-start = (f32[12]{0:T(128)S(1)}, f32[12]{0:T(128)}, u32[]{:S(2)}) copy-start(f32[12]{0:T(128)} %param.13) | copy-start | bytes 148
  1.3 6.2 %copy-start.27 = (s32[1024]{0:T(1024)}, s32[1024]{0:T(1024)S(1)}, u32[]{:S(2)}) copy-start(s32[1024]{0:T(1024)S(1)} %pad_clamp_fusion) | copy-start | bytes 12292
  19.1 68.9 %all-to-all-start = ((bf16[16,2,2,128,256]{4,1,3,2,0:T(2,128)(2,1)}), bf16[16,2,2,128,256]{4,1,3,2,0:T(2,128)(2,1)}, u32[]{:S(2)}, u32[]{:S(2)}) async-start(bf16[16,2,2,128,256]{4,1,3,2,0:T(2,128)(2,1)} %copy.79), calls=%async_computation | async-start | bytes 8388608 | tf_op jit(solution)/shard_map/all_to_all | solution.py:34
  36.3 63.4 %copy-start.3 = (bf16[4,2,256,256]{3,2,1,0:T(8,128)(2,1)S(1)}, bf16[4,2,256,256]{3,2,1,0:T(8,128)(2,1)}, u32[]{:S(2)}) copy-start(bf16[4,2,256,256]{3,2,1,0:T(8,128)(2,1)} %param.10) | copy-start | bytes 3145732
  36.3 63.9 %copy-start.29 = (s32[4,12]{1,0:T(4,128)S(1)}, s32[4,12]{1,0:T(4,128)}, u32[]{:S(2)}) copy-start(s32[4,12]{1,0:T(4,128)} %param.15) | copy-start | bytes 580
  36.3 63.9 %copy-start.19 = (bf16[256,256]{1,0:T(8,128)(2,1)S(1)}, bf16[256,256]{1,0:T(8,128)(2,1)}, u32[]{:S(2)}) copy-start(bf16[256,256]{1,0:T(8,128)(2,1)} %param.11) | copy-start | bytes 393220
  36.3 64.0 %copy-start.17 = (bf16[3,256,256]{2,1,0:T(8,128)(2,1)S(1)}, bf16[3,256,256]{2,1,0:T(8,128)(2,1)}, u32[]{:S(2)}) copy-start(bf16[3,256,256]{2,1,0:T(8,128)(2,1)} %param.12) | copy-start | bytes 1179652
  88.0 63.1 %all-to-all-start.1 = ((bf16[16,2,2,128,256]{4,1,3,2,0:T(2,128)(2,1)}), bf16[16,2,2,128,256]{4,1,3,2,0:T(2,128)(2,1)}, u32[]{:S(2)}, u32[]{:S(2)}) async-start(bf16[16,2,2,128,256]{4,1,3,2,0:T(2,128)(2,1)} %copy.80), calls=%async_computation.1 | async-start | bytes 8388608 | tf_op jit(solution)/shard_map/all_to_all | solution.py:34
  103.0 4.0 copy-start.25
  108.0 3.1 copy-start.15
  173.4 13.1 %copy-start.23 = (f32[4,3,32,1]{2,1,0,3:T(4,128)S(1)}, f32[4,3,32,1]{2,1,0,3:T(4,128)}, u32[]{:S(2)}) copy-start(f32[4,3,32,1]{2,1,0,3:T(4,128)} %convolution_bitcast_fusion.2) | copy-start | bytes 4612
  186.5 9.2 %copy-start.2 = (bf16[32,2,256,256]{3,0,2,1:T(8,128)(2,1)S(1)}, bf16[32,2,256,256]{3,0,2,1:T(8,128)(2,1)}, u32[]{:S(2)}) copy-start(bf16[32,2,256,256]{3,0,2,1:T(8,128)(2,1)} %reshape.55) | copy-start | bytes 25165828
  195.7 2.8 copy-start.21
  211.8 2.2 copy-start.10
  277.2 5.1 %copy-start.26 = (f32[4,24]{1,0:T(4,128)S(1)}, f32[4,24]{1,0:T(4,128)}, u32[]{:S(2)}) copy-start(f32[4,24]{1,0:T(4,128)} %copy-done.25) | copy-start | bytes 1156
  277.2 5.1 %copy-start.31 = (s32[4,24]{1,0:T(4,128)S(1)}, s32[4,24]{1,0:T(4,128)}, u32[]{:S(2)}) copy-start(s32[4,24]{1,0:T(4,128)} %param.17) | copy-start | bytes 1156
  277.2 5.1 %copy-start.32 = (s32[4,24]{1,0:T(4,128)S(1)}, s32[4,24]{1,0:T(4,128)}, u32[]{:S(2)}) copy-start(s32[4,24]{1,0:T(4,128)} %param.16) | copy-start | bytes 1156
  277.2 55.9 %all-to-all-start.3 = ((bf16[16,2,2,128,256]{3,4,2,1,0:T(8,128)(2,1)}), bf16[16,2,2,128,256]{3,4,2,1,0:T(8,128)(2,1)}, u32[]{:S(2)}, u32[]{:S(2)}) async-start(bf16[16,2,2,128,256]{3,4,2,1,0:T(8,128)(2,1)} %get-tuple-element.14), calls=%async_computation.3 | async-start | bytes 8388608 | tf_op jit(solution)/shard_map/all_to_all | solution.py:34
  282.3 2.7 copy-start.16
  341.2 14.8 %copy-start.18 = (bf16[4,2,256,256]{3,0,1,2:T(4,128)(2,1)S(1)}, bf16[4,2,256,256]{3,0,1,2:T(4,128)(2,1)}, u32[]{:S(2)}) copy-start(bf16[4,2,256,256]{3,0,1,2:T(4,128)(2,1)} %copy.106) | copy-start | bytes 3145732
  356.0 5.8 %copy-start.20 = (f32[4,12,32]{2,1,0:T(8,128)S(1)}, f32[4,12,32]{2,1,0:T(8,128)}, u32[]{:S(2)}) copy-start(f32[4,12,32]{2,1,0:T(8,128)} %convolution_multiply_fusion) | copy-start | bytes 18436
  356.0 6.0 %copy-start.28 = (f32[32,4,1,1]{0,1,3,2:T(4,128)S(1)}, f32[32,4,1,1]{0,1,3,2:T(4,128)}, u32[]{:S(2)}) copy-start(f32[32,4,1,1]{0,1,3,2:T(4,128)} %fusion) | copy-start | bytes 1540
  356.0 6.1 %copy-start.4 = (bf16[16,2,2,256,256]{3,4,2,1,0:T(8,128)(2,1)S(1)}, bf16[16,2,2,256,256]{3,4,2,1,0:T(8,128)(2,1)}, u32[]{:S(2)}) copy-start(bf16[16,2,2,256,256]{3,4,2,1,0:T(8,128)(2,1)} %pad_maximum_fusion.1) | copy-start | bytes 25165828
  371.9 7.9 %copy-start.24 = (f32[4,3,32,1]{2,1,0,3:T(4,128)S(1)}, f32[4,3,32,1]{2,1,0,3:T(4,128)}, u32[]{:S(2)}) copy-start(f32[4,3,32,1]{2,1,0,3:T(4,128)} %convolution_bitcast_fusion.2) | copy-start | bytes 4612
  393.9 7.1 %copy-start.6 = (bf16[32,1,256,256]{3,0,2,1:T(8,128)(2,1)S(1)}, bf16[32,1,256,256]{3,0,2,1:T(8,128)(2,1)}, u32[]{:S(2)}) copy-start(bf16[32,1,256,256]{3,0,2,1:T(8,128)(2,1)} %copy.168) | copy-start | bytes 12582916
  394.0 7.1 %copy-start.8 = (f32[4,3,256,256]{3,0,2,1:T(4,128)S(1)}, f32[4,3,256,256]{3,0,2,1:T(4,128)}, u32[]{:S(2)}) copy-start(f32[4,3,256,256]{3,0,2,1:T(4,128)} %fusion.12) | copy-start | bytes 9437188
  394.0 7.1 %copy-start.22 = (f32[4,3,32,1]{2,1,0,3:T(4,128)S(1)}, f32[4,3,32,1]{2,1,0,3:T(4,128)}, u32[]{:S(2)}) copy-start(f32[4,3,32,1]{2,1,0,3:T(4,128)} %convolution_bitcast_fusion.1) | copy-start | bytes 4612
  432.9 7.1 %copy-start.5 = (bf16[32,1,256,256]{3,0,2,1:T(8,128)(2,1)S(1)}, bf16[32,1,256,256]{3,0,2,1:T(8,128)(2,1)}, u32[]{:S(2)}) copy-start(bf16[32,1,256,256]{3,0,2,1:T(8,128)(2,1)} %copy.167) | copy-start | bytes 12582916
  432.9 7.1 %copy-start.7 = (f32[4,3,256,256]{3,0,2,1:T(4,128)S(1)}, f32[4,3,256,256]{3,0,2,1:T(4,128)}, u32[]{:S(2)}) copy-start(f32[4,3,256,256]{3,0,2,1:T(4,128)} %fusion.4) | copy-start | bytes 9437188
  460.8 2.2 copy-start.11
  460.9 2.2 copy-start.12
  463.1 6.3 %copy-start.1 = (f32[12]{0:T(128)S(1)}, f32[12]{0:T(128)}, u32[]{:S(2)}) copy-start(f32[12]{0:T(128)} %param.13) | copy-start | bytes 148
  (4 other events, 5.7 us)
where the time goes:
time: 479 us; the launch traced here: 470 us
  waiting for transfers between devices  128 us (27%)
  local copies, waits for them, and re-layouts  101 us (21%)
  matrix products  89.6 us (19%)
  blocking collectives  88.8 us (19%)
  other arithmetic  35.1 us (7%)
  starting transfers between devices  25.4 us (5%)
    all_to_all x3, waiting for transfers between devices, several_exchanges(): lax.all_to_all(share, axis, split_axis=0, concat_axis=0, tiled=True)  128 us
    all_to_all x1, blocking collectives, several_exchanges(): lax.all_to_all(share, axis, split_axis=0, concat_axis=0, tiled=True)  50.6 us
    psum x4, blocking collectives, over_axes(): value = lax.psum(value, axis)  38.2 us
    reshape x2, local copies, waits for them, and re-layouts, laid_out(): blocks.reshape(*shape[:dim], shape[dim] * shape[dim + 1], *shape[dim + 2:])  27.9 us
    split x4, local copies, waits for them, and re-layouts, several_exchanges(): jnp.split(blocks, cut_rows(blocks.shape[cut], pieces), axis=cut)  25.4 us
    all_to_all x3, starting transfers between devices, several_exchanges(): lax.all_to_all(share, axis, split_axis=0, concat_axis=0, tiled=True)  25.4 us
    unnamed x70, local copies, waits for them, and re-layouts  21.4 us
    concatenate x2, other arithmetic, several_exchanges(): return laid_out(jnp.concatenate(done, axis=cut), concat_dim)  20.5 us
  transfers between devices with their start and end apart: 3, of which 3 were waited for; matrix products, arithmetic and copies ran while one was open for 7% of the time, Pallas kernels for 0%

commit v1 on v0

v1 whole, which is shorter than its diff:
```python
import math

import jax
import jax.numpy as jnp
from jax import lax
from jax.experimental import pallas as pl
from jax.experimental.pallas import tpu as pltpu
from jax.sharding import Mesh
from jax.sharding import PartitionSpec as P


MODES = 12
OPS = 3
NEIGH = 24
NODES = 4
SLOTS = 32
WIDTH = 256
HALF = 128
CHUNKS = 2
PIECE = HALF // CHUNKS
ROWS = 32
HOPS = (2, 1, 3)
LISTS = NODES * OPS * 2
ROOM = (LISTS + 1) * NEIGH
PART = 2 * PIECE
BLOCK = 2 * PART
TIER_MAT = ("tier_0", "tier_1", "mat_0", "mat_1")
SMEM = pltpu.SMEM
ANY = pl.ANY
VMEM_LIMIT = 67043328


def smem():
    return pl.BlockSpec(memory_space=SMEM)


def anywhere():
    return pl.BlockSpec(memory_space=ANY)


def from_offset(value, axis, offset):
    return lax.ppermute(value, axis, [((i + offset) % 4, i) for i in range(4)])


def joint(value, step, cross):
    pairs = []
    for y in range(4):
        for z in range(4):
            for core in range(2):
                if core == cross:
                    to = ((y + step) % 4 * 4 + z) * 2 + core
                else:
                    to = (y * 4 + (z + step) % 4) * 2 + core
                pairs.append(((y * 4 + z) * 2 + core, to))
    return lax.ppermute(value, ("tier_0", "tier_1", "mat_1"), pairs)


def root_of(level):
    high = jnp.where(level == 3, 2.0, math.sqrt(3.0))
    low = jnp.where(level == 1, math.sqrt(2.0), 1.0)
    return jnp.where(level >= 2, high, low).astype(jnp.float32)


def place_of(along, across, s, near):
    return jnp.where(across == 0, along * 4 + near, 16 + (across - 1) * 8 + along * 2 + s)


def position():
    return lax.axis_index("tier_0"), lax.axis_index("tier_1"), lax.axis_index("mat_1")


def prepare_kernel(
    slot,
    mode,
    flag,
    send,
    levels,
    damping,
    coupling,
    hamiltonian,
    couplers,
    counts,
    codes,
    values,
    decay,
    operators,
    table,
):
    for q in range(OPS + 1):
        raw = (hamiltonian[...] if q == 0 else couplers[q - 1]).astype(jnp.float32)
        operators[q * WIDTH : (q + 1) * WIDTH] = ((raw + raw.T) * 0.5).astype(jnp.bfloat16)

    y, z, core = position()
    here = (y * 4 + z) * 2
    for i in range(LISTS + 1):
        counts[i] = 0
    for n in range(NODES):
        rate = levels[n, 0].astype(jnp.float32) * damping[0]
        for k in range(1, MODES):
            rate += levels[n, k].astype(jnp.float32) * damping[k]
        decay[n] = rate

    def tabulate(source, carry):
        dy = lax.rem(source // 4 - y + 4, 4)
        dz = lax.rem(lax.rem(source, 4) - z + 4, 4)
        along = jnp.where(core == 0, dy, dz)
        across = jnp.where(core == 0, dz, dy)
        for s in range(2):
            near = send[along * SLOTS + here + s]
            table[source * 2 + s] = place_of(along, across, s, near)
        return carry

    lax.fori_loop(0, SLOTS // 2, tabulate, 0)

    def step(e, carry):
        for n in range(NODES):
            k = mode[n, e]
            f = flag[n, e]
            j = slot[n, e]
            w = root_of(levels[n, k])
            which = jnp.where(f >= 0, (n * OPS + lax.rem(k, 3)) * 2 + f, LISTS)
            count = counts[which]
            at = which * NEIGH + jnp.where(f >= 0, count, 0)
            counts[which] = count + 1
            codes[at] = table[j]
            codes[ROOM + at] = k
            values[at] = w
            values[ROOM + at] = w * coupling[0, k]
            values[2 * ROOM + at] = w * coupling[1, k]
        return carry

    lax.fori_loop(0, NEIGH, step, 0)


def prepare(slot, mode, flag, send, levels, damping, coupling, hamiltonian, couplers):
    return pl.pallas_call(
        prepare_kernel,
        out_shape=(
            jax.ShapeDtypeStruct((LISTS + 1,), jnp.int32),
            jax.ShapeDtypeStruct((2 * ROOM,), jnp.int32),
            jax.ShapeDtypeStruct((3 * ROOM,), jnp.float32),
            jax.ShapeDtypeStruct((NODES,), jnp.float32),
            jax.ShapeDtypeStruct(((OPS + 1) * WIDTH, WIDTH), jnp.bfloat16),
        ),
        in_specs=[smem()] * 7 + [pl.BlockSpec(memory_space=pltpu.VMEM)] * 2,
        out_specs=(smem(),) * 4 + (pl.BlockSpec(memory_space=pltpu.VMEM),),
        scratch_shapes=[SMEM((SLOTS,), jnp.int32)],
        cost_estimate=pl.CostEstimate(flops=2000000, bytes_accessed=20000, transcendentals=0),
        name="prepare",
    )(slot, mode, flag, send, levels, damping, coupling, hamiltonian, couplers)


def copy_through(reads, writes):
    for read in reads:
        read.start()
    for read, write in zip(reads, writes):
        read.wait()
        write.start()
    for write in writes:
        write.wait()


def across(hop):
    y, z, core = position()
    along_z = y * 4 + lax.rem(z + hop, 4)
    along_y = lax.rem(y + hop, 4) * 4 + z
    return jnp.where(core == 0, along_z, along_y) * 2


def pick_kernel(send, *refs):
    ins = refs[0:4]
    outs = refs[4:7]
    room, in_sem, out_sem = refs[7:]
    reads = []
    writes = []
    for i, hop in enumerate(HOPS):
        there = across(hop)
        for d in range(4):
            for s in range(2):
                at = d * 2 + s
                slot = i * 8 + at
                row = pl.multiple_of(send[d * SLOTS + there + s] * BLOCK, BLOCK)
                reads.append(
                    pltpu.make_async_copy(
                        ins[d].at[pl.ds(row, BLOCK)], room.at[slot], in_sem.at[slot]
                    )
                )
                writes.append(
                    pltpu.make_async_copy(room.at[slot], outs[i].at[at], out_sem.at[slot])
                )
    copy_through(reads, writes)


def pick(send, parts):
    shape = jax.ShapeDtypeStruct((8, BLOCK, WIDTH), jnp.bfloat16)
    return pl.pallas_call(
        pick_kernel,
        out_shape=(shape,) * 3,
        in_specs=[smem()] + [anywhere()] * 4,
        out_specs=(anywhere(),) * 3,
        scratch_shapes=[
            pltpu.VMEM((24, BLOCK, WIDTH), jnp.bfloat16),
            pltpu.SemaphoreType.DMA((24,)),
            pltpu.SemaphoreType.DMA((24,)),
        ],
        compiler_params=pltpu.CompilerParams(vmem_limit_bytes=VMEM_LIMIT),
        cost_estimate=pl.CostEstimate(flops=3000000, bytes_accessed=6 << 20, transcendentals=0),
        name="pick",
    )(send, *parts)


def row_of(chunk, half):
    return chunk * 2 * PIECE + half * PIECE


def rate_kernel(chunk, last, counts, codes, values, decay, operators_from, *refs):
    final = chunk == CHUNKS - 1
    own_from = refs[0:CHUNKS]
    refs = refs[CHUNKS:]
    if chunk > 0:
        before_from = refs[0]
        refs = refs[1:]
    sources = refs[0:7]
    refs = refs[7:]
    outs = CHUNKS if final and not last else 1
    out = refs[0:outs]
    grads, buffer, left, right, held, totals, sems, own, operators, *rest = refs[outs:]
    n = pl.program_id(0)

    copies = ([], [])
    for half in range(2):
        moves = []
        rows = pl.ds(half * PART, PART)
        for part in range(7):
            ref = sources[part]
            if part < 4:
                for m in range(NODES):
                    from_rows = pl.ds(m * BLOCK + half * PART, PART)
                    moves.append((ref.at[from_rows], buffer.at[part * 4 + m, rows]))
            else:
                places = pl.ds(16 + (part - 4) * 8, 8)
                moves.append((ref.at[:, rows], buffer.at[places, rows]))
        for i, (ref, to) in enumerate(moves):
            copies[half].append(pltpu.make_async_copy(ref, to, sems.at[half * 19 + i]))

    own_copies = [
        pltpu.make_async_copy(
            own_from[c].at[pl.ds(0, NODES * BLOCK)], own.at[c], sems.at[38 + c]
        )
        for c in range(CHUNKS)
    ]
    late_copies = [pltpu.make_async_copy(operators_from, operators, sems.at[38 + CHUNKS])]
    if chunk > 0:
        before = rest[0]
        late_copies.append(pltpu.make_async_copy(before_from, before, sems.at[39 + CHUNKS]))

    @pl.when(n == 0)
    def _():
        for copy in own_copies + copies[0] + copies[1] + late_copies:
            copy.start()
        totals[...] = jnp.zeros_like(totals)

    for half in range(2):
        mine = own.at[chunk, pl.ds(pl.multiple_of(n * BLOCK, BLOCK), BLOCK)]
        base = half * PART

        @pl.when(n == 0)
        def _(half=half):
            for copy in own_copies * (half == 0) + copies[half]:
                copy.wait()

        def block(i, carry, half=half, mine=mine, base=base):
            row = pl.multiple_of(i * ROWS, ROWS)
            here = pl.multiple_of(half * PIECE + i * ROWS, ROWS)
            own_real = mine[pl.ds(base + row, ROWS), :].astype(jnp.float32)
            own_imag = mine[pl.ds(base + PIECE + row, ROWS), :].astype(jnp.float32)
            held[0] = own_real
            held[1] = own_imag
            zero = jnp.zeros((ROWS, WIDTH), jnp.float32)
            left[0, pl.ds(here, ROWS), :] = (-own_imag).astype(jnp.bfloat16)
            left[1, pl.ds(here, ROWS), :] = own_real.astype(jnp.bfloat16)
            right[0, pl.ds(here, ROWS), 0:WIDTH] = (-own_imag).astype(jnp.bfloat16)
            right[1, pl.ds(here, ROWS), 0:WIDTH] = own_real.astype(jnp.bfloat16)
            for q in range(OPS):

                def entry(at):
                    place = codes[at]
                    mode = codes[ROOM + at]
                    return place, mode, values[at], values[ROOM + at], values[2 * ROOM + at]

                def load(now):
                    place, mode, w, u, v = now
                    real = buffer[place, pl.ds(half * PART + row, ROWS), :].astype(jnp.float32)
                    imag = buffer[place, pl.ds(half * PART + PIECE + row, ROWS), :].astype(jnp.float32)
                    product = held[0] * real + held[1] * imag
                    product = product[:, 0:128] + product[:, 128:256]
                    product = jnp.sum(product.reshape(ROWS // 8, 8, 128), axis=0)
                    totals[mode] = totals[mode] + w * product
                    return real, imag, u, v

                which = (n * OPS + q) * 2

                def raised(e, carry):
                    now, sum_real, sum_imag = carry
                    after = entry((which + 1) * NEIGH + e + 1)
                    real, imag, u, v = load(now)
                    return (
                        after,
                        sum_real + (u * real - v * imag),
                        sum_imag + (u * imag + v * real),
                    )

                def lowered(e, carry):
                    now, sum_real, sum_imag, turn_real, turn_imag = carry
                    after = entry(which * NEIGH + e + 1)
                    real, imag, u, v = load(now)
                    return (
                        after,
                        sum_real + u * real,
                        sum_imag + u * imag,
                        turn_real + v * real,
                        turn_imag + v * imag,
                    )

                start = entry((which + 1) * NEIGH)
                start_lowered = entry(which * NEIGH)
                _, sum_real, sum_imag = lax.fori_loop(
                    0, counts[which + 1], raised, (start, zero, zero)
                )
                _, sum_real, sum_imag, turn_real, turn_imag = lax.fori_loop(
                    0, counts[which], lowered, (start_lowered, sum_real, sum_imag, zero, zero)
                )
                at_row = pl.multiple_of((q + 1) * 2 * PIECE + here, ROWS)
                column = (q + 1) * WIDTH
                left[0, pl.ds(at_row, ROWS), :] = (sum_real - turn_imag).astype(jnp.bfloat16)
                left[1, pl.ds(at_row, ROWS), :] = (sum_imag + turn_real).astype(jnp.bfloat16)
                right[0, pl.ds(here, ROWS), column : column + WIDTH] = (
                    sum_real + turn_imag
                ).astype(jnp.bfloat16)
                right[1, pl.ds(here, ROWS), column : column + WIDTH] = (
                    sum_imag - turn_real
                ).astype(jnp.bfloat16)
            return carry

        lax.fori_loop(0, PIECE // ROWS, block, 0)

    @pl.when(n == 0)
    def _():
        for copy in late_copies:
            copy.wait()

    rate_decay = decay[n]
    columns = slice(chunk * 2 * PIECE, (chunk + 1) * 2 * PIECE)
    op_left = jnp.concatenate(
        [operators[q * WIDTH : (q + 1) * WIDTH, columns] for q in range(OPS + 1)], axis=1
    )
    for part in range(2):
        total = jnp.dot(op_left, left[part], preferred_element_type=jnp.float32)
        minus = jnp.dot(right[part], operators[...], preferred_element_type=jnp.float32)
        if chunk > 0:
            total += before[n, part]
        for c in range(CHUNKS):
            for half in range(2):
                rows = slice(row_of(c, half), row_of(c, half) + PIECE)
                value = total[rows]
                if c == chunk or (final and not last):
                    at = half * PART + part * PIECE
                    state = own[c, pl.ds(pl.multiple_of(n * BLOCK + at, PIECE), PIECE)].astype(
                        jnp.float32
                    )
                if c == chunk:
                    value -= minus[half * PIECE : (half + 1) * PIECE] + rate_decay * state
                if not final:
                    out[0][0, part, rows] = value
                elif last:
                    out[0][0, part, rows] = 0.25 * value
                else:
                    out[c][at : at + PIECE] = (state + 0.125 * value).astype(jnp.bfloat16)

    @pl.when(n == NODES - 1)
    def _():
        summed = jnp.sum(totals[...], axis=1)
        summed = jnp.sum(summed, axis=1, keepdims=True) * (1.0 / WIDTH)
        grads[...] = jnp.broadcast_to(summed, (MODES, 128))


def rates(chunk, last, lists, decay, operators, own, before, sources):
    final = chunk == CHUNKS - 1
    counts, codes, values = lists
    whole = pl.BlockSpec((1, 2, WIDTH, WIDTH), lambda n: (n, 0, 0, 0))
    block = pl.BlockSpec((BLOCK, WIDTH), lambda n: (n, 0))
    if final and not last:
        outs = (jax.ShapeDtypeStruct((NODES * BLOCK, WIDTH), jnp.bfloat16),) * CHUNKS
        out_specs = (block,) * CHUNKS
    else:
        outs = (jax.ShapeDtypeStruct((NODES, 2, WIDTH, WIDTH), jnp.float32),)
        out_specs = (whole,)
    return pl.pallas_call(
        lambda *refs: rate_kernel(chunk, last, *refs),
        grid=(NODES,),
        out_shape=outs + (jax.ShapeDtypeStruct((MODES, 128), jnp.float32),),
        in_specs=[smem()] * 4
        + [anywhere()] * (8 + CHUNKS + (chunk > 0)),
        out_specs=out_specs + (pl.BlockSpec((MODES, 128), lambda n: (0, 0)),),
        scratch_shapes=[
            pltpu.VMEM((40, 2 * PART, WIDTH), jnp.bfloat16),
            pltpu.VMEM((2, (OPS + 1) * 2 * PIECE, WIDTH), jnp.bfloat16),
            pltpu.VMEM((2, 2 * PIECE, (OPS + 1) * WIDTH), jnp.bfloat16),
            pltpu.VMEM((2, ROWS, WIDTH), jnp.float32),
            pltpu.VMEM((MODES, 8, 128), jnp.float32),
            pltpu.SemaphoreType.DMA((40 + CHUNKS,)),
            pltpu.VMEM((CHUNKS, NODES * BLOCK, WIDTH), jnp.bfloat16),
            pltpu.VMEM(operators.shape, jnp.bfloat16),
        ]
        + [pltpu.VMEM((NODES, 2, WIDTH, WIDTH), jnp.float32)] * (chunk > 0),
        compiler_params=pltpu.CompilerParams(
            vmem_limit_bytes=VMEM_LIMIT, dimension_semantics=("arbitrary",)
        ),
        cost_estimate=pl.CostEstimate(
            flops=2 * 2 * 4 * 4 * WIDTH**3, bytes_accessed=8 << 20, transcendentals=0
        ),
        name="rates",
    )(counts, codes, values, decay, operators, *own, *before, *sources)


def over_all(value):
    value = value + lax.ppermute(value, "mat_1", [(0, 1), (1, 0)])
    for axis in ("mat_0", "tier_1", "tier_0"):
        one = from_offset(value, axis, 1)
        three = from_offset(value, axis, 3)
        two = from_offset(value, axis, 2)
        value = (value + two) + (one + three)
    return value


def per_device(
    costate,
    hamiltonian,
    couplers,
    damping,
    coupling,
    levels,
    neighbour_slot,
    neighbour_mode,
    neighbour_flag,
    send_index,
):
    split = costate.reshape(NODES, 2, CHUNKS, 2, PIECE, WIDTH).transpose(2, 0, 3, 1, 4, 5)
    split = split.reshape(CHUNKS, NODES * BLOCK, WIDTH)
    label = jnp.pad(send_index.astype(jnp.bfloat16), ((0, 15), (0, WIDTH - SLOTS)))
    start = [jnp.concatenate([split[0], label])] + [split[c] for c in range(1, CHUNKS)]

    def section(own, last, tables):
        rings = []
        for c in range(CHUNKS):
            parts = [own[c]] * 4
            for offset in (2, 1, 3):
                parts[offset] = joint(own[c], 4 - offset, 0)
            rings.append(parts)
        if tables is None:
            held = lax.optimization_barrier(rings[0])
            send = jnp.concatenate([part[NODES * BLOCK, :SLOTS] for part in held]).astype(jnp.int32)
            *lists, decay, operators = prepare(
                neighbour_slot,
                neighbour_mode,
                neighbour_flag,
                send,
                levels,
                damping,
                coupling,
                hamiltonian,
                couplers,
            )
            tables = (send, lists, decay, operators)
        send, lists, decay, operators = tables
        far = []
        for c in range(CHUNKS):
            picked = pick(send, rings[c])
            come = {}
            for i, hop in enumerate(HOPS):
                come[4 - hop] = joint(picked[i], hop, 1)
            far.append(come)
        grads = 0.0
        before = ()
        for c in range(CHUNKS):
            sources = rings[c] + [far[c][d] for d in (1, 2, 3)]
            *before, grad = rates(c, last, lists, decay, operators, own, before, sources)
            grads = grads + grad
        return before, grads, tables

    middle, grad_first, tables = section(start, False, None)
    (increment,), grad_second, _ = section(middle, True, tables)
    gradient = over_all(grad_first + grad_second)
    return (increment, gradient[:, 0])


def solution(mesh):
    finer = Mesh(mesh.devices.reshape(4, 4, 4, 2), TIER_MAT)
    return jax.shard_map(
        per_device,
        mesh=finer,
        in_specs=(
            P(TIER_MAT, None, None, None),
            P(),
            P(),
            P(),
            P(),
            P(TIER_MAT, None),
            P(TIER_MAT, None),
            P(TIER_MAT, None),
            P(TIER_MAT, None),
            P(TIER_MAT, None),
        ),
        out_specs=(P(TIER_MAT, None, None, None), P()),
        check_vma=False,
    )
```

time: 479 us -> 242 us (0.51)
  local copies, waits for them, and re-layouts: 101 us -> 3.03 us
  matrix products: 89.6 us -> 0 us
  blocking collectives: 88.8 us -> 0 us
  Pallas kernels: 0 us -> 77.9 us
  other arithmetic: 35.1 us -> 2.68 us
  waiting for transfers between devices: 128 us -> 108 us
  starting transfers between devices: 25.4 us -> 44.5 us
    all_to_all x3 -> x0, waiting for transfers between devices: 128 us -> none  [several_exchanges(): lax.all_to_all(share, axis, split_axis=0, concat_axis=0, tiled=True)]
    ppermute x0 -> x34, waiting for transfers between devices: none -> 108 us  [the longest x24 102 us: joint(): return lax.ppermute(value, ('tier_0', 'tier_1', 'mat_1'), pairs)]
    dot_general x32 -> x0, matrix products: 89.6 us -> none  [the longest x4 17.2 us: combine(): jnp.einsum('nqs,sij->nqij', cimag, received_f[:, 1], precision=high)]
    pallas_call x0 -> x9, Pallas kernels: none -> 77.9 us  [the longest x4 55.7 us: rates(): pl.pallas_call(lambda *refs: rate_kernel(chunk, last, *refs), grid=(NODES...]
    all_to_all x1 -> x0, blocking collectives: 50.6 us -> none  [several_exchanges(): lax.all_to_all(share, axis, split_axis=0, concat_axis=0, tiled=True)]
    ppermute x0 -> x34, starting transfers between devices: none -> 44.5 us  [the longest x24 22.7 us: joint(): return lax.ppermute(value, ('tier_0', 'tier_1', 'mat_1'), pairs)]
    psum x4 -> x0, blocking collectives: 38.2 us -> none  [over_axes(): value = lax.psum(value, axis)]
    reshape x2 -> x1, local copies, waits for them, and re-layouts: 27.9 us -> 1.29 us  [per_device(): costate.reshape(NODES, 2, CHUNKS, 2, PIECE, WIDTH)]
  transfers between devices with their start and end apart: 3 -> 34, of which waited for: 3 -> 20; matrix products, arithmetic and copies ran while one was open for 7% -> 0% of each run, Pallas kernels for 0% -> 17%
where the time goes in v1:
time: 242 us; the launch traced here: 237 us
  waiting for transfers between devices  108 us (45%)
  Pallas kernels  77.9 us (32%)
  starting transfers between devices  44.5 us (18%)
  local copies, waits for them, and re-layouts  3.03 us (1%)
  other arithmetic  2.68 us (1%)
    ppermute x24, waiting for transfers between devices, joint(): return lax.ppermute(value, ('tier_0', 'tier_1', 'mat_1'), pairs)  102 us
    pallas_call x4, Pallas kernels, rates(): pl.pallas_call(lambda *refs: rate_kernel(chunk, last, *refs), grid=(NODES...  55.7 us
    ppermute x24, starting transfers between devices, joint(): return lax.ppermute(value, ('tier_0', 'tier_1', 'mat_1'), pairs)  22.7 us
    pallas_call x4, Pallas kernels, pick(): pl.pallas_call(pick_kernel, out_shape=(shape,) * 3, in_specs=[smem()] + [...  18.2 us
    ppermute x9, starting transfers between devices, from_offset(): return lax.ppermute(value, axis, [((i + offset) % 4, i) for i in range(4)])  14.7 us
    ppermute x1, starting transfers between devices, over_all(): value = value + lax.ppermute(value, 'mat_1', [(0, 1), (1, 0)])  7.09 us
    ppermute x9, waiting for transfers between devices, from_offset(): return lax.ppermute(value, axis, [((i + offset) % 4, i) for i in range(4)])  5.88 us
  transfers between devices with their start and end apart: 34, of which 20 were waited for; matrix products, arithmetic and copies ran while one was open for 0% of the time, Pallas kernels for 17%

profile of v1, /device:TPU:1, one launch (start us, length us, event | category | flops | bytes accessed | tf_op | source)
XLA Modules:
  0.0 237.4 jit_solution(4065159509764275008)
XLA Ops:
  3.5 4.6 %collective-permute-start = (bf16[1040,256]{1,0:T(8,128)(2,1)S(1)}, bf16[1040,256]{1,0:T(8,128)(2,1)S(1)}, u32[]{:S(2)}, u32[]{:S(2)}) collective-permute-start(bf16[1040,256]{1,0:T(8,128)(2,1)S(1)} %fusion.1.refs_0_.refs_5_.refs_7_), channel_id=1, source_target_pairs={{0,96},{1,25},{8,104},{9,1},{16,112},{17,9},{24,120},{25,17},{32,0... | collective-permute-start | bytes 1597448 | tf_op jit(solution)/shard_map/ppermute | solution.py:55
  8.9 11.2 %collective-permute-done.refs_1_.refs_8_ = bf16[1040,256]{1,0:T(8,128)(2,1)S(1)} collective-permute-done((bf16[1040,256]{1,0:T(8,128)(2,1)S(1)}, bf16[1040,256]{1,0:T(8,128)(2,1)S(1)}, u32[]{:S(2)}, u32[]{:S(2)}) %collective-permute-start) | collective-permute-done | bytes 532512 | tf_op jit(solution)/shard_map/ppermute | solution.py:55
  20.1 3.4 %collective-permute-done.2.refs_3_.refs_10_ = bf16[1040,256]{1,0:T(8,128)(2,1)S(1)} collective-permute-done((bf16[1040,256]{1,0:T(8,128)(2,1)S(1)}, bf16[1040,256]{1,0:T(8,128)(2,1)S(1)}, u32[]{:S(2)}, u32[]{:S(2)}) %collective-permute-start.2) | collective-permute-done | bytes 532512 | tf_op jit(solution)/shard_map/ppermute | solution.py:55
  25.0 4.7 %pick.4 = (bf16[8,256,256]{2,1,0:T(8,128)(2,1)}, bf16[8,256,256]{2,1,0:T(8,128)(2,1)}, bf16[8,256,256]{2,1,0:T(8,128)(2,1)}) custom-call(s32[128]{0:T(128)} %maximum_convert_fusion.send, bf16[1040,256]{1,0:T(8,128)(2,1)} %copy-done, bf16[1040,256]{1,0:T(8,128)(2,1)} %copy-done.1, bf16[1040,256]{1,0:T(8,128)(2,1)} %copy-done.2, bf16[1040,256]{1,0:T(8,128)(2,1)} %copy-done.3), custom_call_target="tpu_custom_call" | custom-call | flops 3000000 | bytes 6291456 | tf_op jit(solution)/shard_map/pick/pallas_call | solution.py:196
  29.6 2.4 %collective-permute-start.3 = (bf16[8,256,256]{2,1,0:T(8,128)(2,1)}, bf16[8,256,256]{2,1,0:T(8,128)(2,1)}, u32[]{:S(2)}, u32[]{:S(2)}) collective-permute-start(bf16[8,256,256]{2,1,0:T(8,128)(2,1)} %get-tuple-element.41), channel_id=1, source_target_pairs={{0,24},{1,97},{8,0},{9,105},{16,8},{17,113},{24,16},{25,121},{32,5... | collective-permute-start | bytes 3145736 | tf_op jit(solution)/shard_map/ppermute | solution.py:55
  34.0 12.2 %collective-permute-done.6.refs_1_.refs_9_ = bf16[1024,256]{1,0:T(8,128)(2,1)} collective-permute-done((bf16[1024,256]{1,0:T(8,128)(2,1)}, bf16[1024,256]{1,0:T(8,128)(2,1)}, u32[]{:S(2)}, u32[]{:S(2)}) %collective-permute-start.6) | collective-permute-done | bytes 524320 | tf_op jit(solution)/shard_map/ppermute | solution.py:55
  46.3 14.1 %collective-permute-done.8.refs_3_.refs_11_ = bf16[1024,256]{1,0:T(8,128)(2,1)} collective-permute-done((bf16[1024,256]{1,0:T(8,128)(2,1)}, bf16[1024,256]{1,0:T(8,128)(2,1)}, u32[]{:S(2)}, u32[]{:S(2)}) %collective-permute-start.8) | collective-permute-done | bytes 524320 | tf_op jit(solution)/shard_map/ppermute | solution.py:55
  60.4 4.5 %pick.5 = (bf16[8,256,256]{2,1,0:T(8,128)(2,1)}, bf16[8,256,256]{2,1,0:T(8,128)(2,1)}, bf16[8,256,256]{2,1,0:T(8,128)(2,1)}) custom-call(s32[128]{0:T(128)} %maximum_convert_fusion.send, bf16[1024,256]{1,0:T(8,128)(2,1)} %bitcast.17, bf16[1024,256]{1,0:T(8,128)(2,1)} %collective-permute-done.6.refs_1_.refs_9_, ...), custom_call_target="tpu_custom_call" | custom-call | flops 3000000 | bytes 6291456 | tf_op jit(solution)/shard_map/pick/pallas_call | solution.py:196
  65.1 1.5 collective-permute-done.3.refs_11_
  66.6 4.0 %prepare.1 = (s32[25]{0:T(128)}, s32[1200]{0:T(1024)}, f32[1800]{0:T(1024)}, f32[4]{0:T(128)}, bf16[1024,256]{1,0:T(8,128)(2,1)}) custom-call(s32[4,24]{1,0:T(4,128)} %slot.1, s32[4,24]{1,0:T(4,128)} %mode.1, s32[4,24]{1,0:T(4,128)} %flag.1, s32[128]{0:T(128)} %maximum_convert_fusion.send, s32[4,12]{1,0:T(4,128)} %levels.1, f32[12]{0:T(128)} %damping.1, ...), custom_call_target="tpu_custom_call" | custom-call | flops 2000000 | bytes 20000 | tf_op jit(solution)/shard_map/prepare/pallas_call | solution.py:136
  71.5 13.9 %rates.4 = (f32[4,2,256,256]{3,2,1,0:T(8,128)}, f32[12,128]{1,0:T(8,128)}) custom-call(s32[25]{0:T(128)} %get-tuple-element.36.refs_0_, s32[1200]{0:T(1024)} %get-tuple-element.37.refs_1_, f32[1800]{0:T(1024)} %get-tuple-element.38.refs_2_, f32[4]{0:T(128)} %get-tuple-element.39.refs_3_, bf16[1024,256]{1,0:T(8,128)(2,1)} %get-tuple-element.40.refs_4_, ...), custom_call_target="tpu_custom_call" | custom-call | flops 1073741824 | bytes 8388608 | tf_op jit(solution)/shard_map/rates/pallas_call | solution.py:398
  85.4 8.9 %collective-permute-done.11.refs_14_ = bf16[8,256,256]{2,1,0:T(8,128)(2,1)} collective-permute-done((bf16[8,256,256]{2,1,0:T(8,128)(2,1)}, bf16[8,256,256]{2,1,0:T(8,128)(2,1)}, u32[]{:S(2)}, u32[]{:S(2)}) %collective-permute-start.11) | collective-permute-done | bytes 1048608 | tf_op jit(solution)/shard_map/ppermute | solution.py:55
  94.3 13.9 %rates.5 = (bf16[1024,256]{1,0:T(8,128)(2,1)}, bf16[1024,256]{1,0:T(8,128)(2,1)}, f32[12,128]{1,0:T(8,128)}) custom-call(s32[25]{0:T(128)} %get-tuple-element.36.refs_0_, s32[1200]{0:T(1024)} %get-tuple-element.37.refs_1_, f32[1800]{0:T(1024)} %get-tuple-element.38.refs_2_, f32[4]{0:T(128)} %get-tuple-element.39.refs_3_, ...), custom_call_target="tpu_custom_call" | custom-call | flops 1073741824 | bytes 8388608 | tf_op jit(solution)/shard_map/rates/pallas_call | solution.py:398
  108.2 3.1 %collective-permute-start.12 = (bf16[1024,256]{1,0:T(8,128)(2,1)}, bf16[1024,256]{1,0:T(8,128)(2,1)}, u32[]{:S(2)}, u32[]{:S(2)}) collective-permute-start(bf16[1024,256]{1,0:T(8,128)(2,1)} %get-tuple-element.48.refs_0_.refs_5_.refs_7_), channel_id=1, source_target_pairs={{0,96},{1,25},{8,104},{9,1},{16,112},{17,9},{24,120},{25,17},{32,0... | collective-permute-start | bytes 1572872 | tf_op jit(solution)/shard_map/ppermute | solution.py:55
  111.9 11.4 %collective-permute-done.12.refs_1_.refs_8_ = bf16[1024,256]{1,0:T(8,128)(2,1)} collective-permute-done((bf16[1024,256]{1,0:T(8,128)(2,1)}, bf16[1024,256]{1,0:T(8,128)(2,1)}, u32[]{:S(2)}, u32[]{:S(2)}) %collective-permute-start.12) | collective-permute-done | bytes 524320 | tf_op jit(solution)/shard_map/ppermute | solution.py:55
  123.3 3.4 %collective-permute-done.14.refs_3_.refs_10_ = bf16[1024,256]{1,0:T(8,128)(2,1)} collective-permute-done((bf16[1024,256]{1,0:T(8,128)(2,1)}, bf16[1024,256]{1,0:T(8,128)(2,1)}, u32[]{:S(2)}, u32[]{:S(2)}) %collective-permute-start.14) | collective-permute-done | bytes 524320 | tf_op jit(solution)/shard_map/ppermute | solution.py:55
  126.7 4.5 %pick.6 = (bf16[8,256,256]{2,1,0:T(8,128)(2,1)}, bf16[8,256,256]{2,1,0:T(8,128)(2,1)}, bf16[8,256,256]{2,1,0:T(8,128)(2,1)}) custom-call(s32[128]{0:T(128)} %maximum_convert_fusion.send, bf16[1024,256]{1,0:T(8,128)(2,1)} %get-tuple-element.48.refs_0_.refs_5_.refs_7_, bf16[1024,256]{1,0:T(8,128)(2,1)} %collective-permute-done.12.refs_1_.refs_8_, ...), custom_call_target="tpu_custom_call" | custom-call | flops 3000000 | bytes 6291456 | tf_op jit(solution)/shard_map/pick/pallas_call | solution.py:196
  133.2 6.5 %collective-permute-done.18.refs_1_.refs_9_ = bf16[1024,256]{1,0:T(8,128)(2,1)} collective-permute-done((bf16[1024,256]{1,0:T(8,128)(2,1)}, bf16[1024,256]{1,0:T(8,128)(2,1)}, u32[]{:S(2)}, u32[]{:S(2)}) %collective-permute-start.18) | collective-permute-done | bytes 524320 | tf_op jit(solution)/shard_map/ppermute | solution.py:55
  139.7 4.7 %collective-permute-start.17 = (bf16[8,256,256]{2,1,0:T(8,128)(2,1)}, bf16[8,256,256]{2,1,0:T(8,128)(2,1)}, u32[]{:S(2)}, u32[]{:S(2)}) collective-permute-start(bf16[8,256,256]{2,1,0:T(8,128)(2,1)} %get-tuple-element.52), channel_id=1, source_target_pairs={{0,8},{1,33},{8,16},{9,41},{16,24},{17,49},{24,0},{25,57},{32,40},... | collective-permute-start | bytes 3145736 | tf_op jit(solution)/shard_map/ppermute | solution.py:55
  144.4 7.1 %collective-permute-done.20.refs_3_.refs_11_ = bf16[1024,256]{1,0:T(8,128)(2,1)} collective-permute-done((bf16[1024,256]{1,0:T(8,128)(2,1)}, bf16[1024,256]{1,0:T(8,128)(2,1)}, u32[]{:S(2)}, u32[]{:S(2)}) %collective-permute-start.20) | collective-permute-done | bytes 524320 | tf_op jit(solution)/shard_map/ppermute | solution.py:55
  151.5 4.6 %pick.7 = (bf16[8,256,256]{2,1,0:T(8,128)(2,1)}, bf16[8,256,256]{2,1,0:T(8,128)(2,1)}, bf16[8,256,256]{2,1,0:T(8,128)(2,1)}) custom-call(s32[128]{0:T(128)} %maximum_convert_fusion.send, bf16[1024,256]{1,0:T(8,128)(2,1)} %get-tuple-element.49.refs_6_.refs_0_.refs_8_, bf16[1024,256]{1,0:T(8,128)(2,1)} %collective-permute-done.18.refs_1_.refs_9_, ...), custom_call_target="tpu_custom_call" | custom-call | flops 3000000 | bytes 6291456 | tf_op jit(solution)/shard_map/pick/pallas_call | solution.py:196
  156.2 2.3 collective-permute-start.22
  158.5 12.3 %collective-permute-done.17.refs_13_ = bf16[8,256,256]{2,1,0:T(8,128)(2,1)} collective-permute-done((bf16[8,256,256]{2,1,0:T(8,128)(2,1)}, bf16[8,256,256]{2,1,0:T(8,128)(2,1)}, u32[]{:S(2)}, u32[]{:S(2)}) %collective-permute-start.17) | collective-permute-done | bytes 1048608 | tf_op jit(solution)/shard_map/ppermute | solution.py:55
  170.8 13.9 %rates.6 = (f32[4,2,256,256]{3,2,1,0:T(8,128)}, f32[12,128]{1,0:T(8,128)}) custom-call(s32[25]{0:T(128)} %get-tuple-element.36.refs_0_, s32[1200]{0:T(1024)} %get-tuple-element.37.refs_1_, f32[1800]{0:T(1024)} %get-tuple-element.38.refs_2_, f32[4]{0:T(128)} %get-tuple-element.39.refs_3_, bf16[1024,256]{1,0:T(8,128)(2,1)} %get-tuple-element.40.refs_4_, ...), custom_call_target="tpu_custom_call" | custom-call | flops 1073741824 | bytes 8388608 | tf_op jit(solution)/shard_map/rates/pallas_call | solution.py:398
  184.7 8.8 %collective-permute-done.23.refs_14_ = bf16[8,256,256]{2,1,0:T(8,128)(2,1)} collective-permute-done((bf16[8,256,256]{2,1,0:T(8,128)(2,1)}, bf16[8,256,256]{2,1,0:T(8,128)(2,1)}, u32[]{:S(2)}, u32[]{:S(2)}) %collective-permute-start.23) | collective-permute-done | bytes 1048608 | tf_op jit(solution)/shard_map/ppermute | solution.py:55
  193.6 14.0 %rates.7 = (f32[4,2,256,256]{3,2,1,0:T(8,128)}, f32[12,128]{1,0:T(8,128)}) custom-call(s32[25]{0:T(128)} %get-tuple-element.36.refs_0_, s32[1200]{0:T(1024)} %get-tuple-element.37.refs_1_, f32[1800]{0:T(1024)} %get-tuple-element.38.refs_2_, f32[4]{0:T(128)} %get-tuple-element.39.refs_3_, bf16[1024,256]{1,0:T(8,128)(2,1)} %get-tuple-element.40.refs_4_, ...), custom_call_target="tpu_custom_call" | custom-call | flops 1073741824 | bytes 8388608 | tf_op jit(solution)/shard_map/rates/pallas_call | solution.py:398
  208.3 7.1 %collective-permute-start.24 = (f32[12,128]{1,0:T(8,128)S(1)}, f32[12,128]{1,0:T(8,128)S(1)}, u32[]{:S(2)}, u32[]{:S(2)}) collective-permute-start(f32[12,128]{1,0:T(8,128)S(1)} %add_add_fusion.2), channel_id=1, source_target_pairs={{0,1},{1,0},{2,3},{3,2},{4,5},{5,4},{6,7},{7,6},{8,9},{9,8},{10,11... | collective-permute-start | bytes 18440 | tf_op jit(solution)/shard_map/ppermute | solution.py:427
  217.7 3.0 %collective-permute-start.25 = (f32[12,128]{1,0:T(8,128)S(1)}, f32[12,128]{1,0:T(8,128)S(1)}, u32[]{:S(2)}, u32[]{:S(2)}) collective-permute-start(f32[12,128]{1,0:T(8,128)S(1)} %add.44), channel_id=1, source_target_pairs={{4,0},{6,2},{0,4},{2,6},{5,1},{7,3},{1,5},{3,7},{12,8},{14,10},{8,... | collective-permute-start | bytes 18440 | tf_op jit(solution)/shard_map/ppermute | solution.py:42
  223.3 1.4 collective-permute-start.28
  224.7 1.5 collective-permute-done.30
  227.3 5.5 %collective-permute-start.33 = (f32[12,128]{1,0:T(8,128)S(1)}, f32[12,128]{1,0:T(8,128)S(1)}, u32[]{:S(2)}, u32[]{:S(2)}) collective-permute-start(f32[12,128]{1,0:T(8,128)S(1)} %add_add_fusion), channel_id=1, source_target_pairs={{96,0},{0,32},{32,64},{64,96},{97,1},{1,33},{33,65},{65,97},{98,2}... | collective-permute-start | bytes 18440 | tf_op jit(solution)/shard_map/ppermute | solution.py:42
  232.8 1.9 collective-permute-start.31
  (65 shorter events, 20.4 us)
Async XLA Ops:
  3.5 16.6 %collective-permute-start = (bf16[1040,256]{1,0:T(8,128)(2,1)S(1)}, bf16[1040,256]{1,0:T(8,128)(2,1)S(1)}, u32[]{:S(2)}, u32[]{:S(2)}) collective-permute-start(bf16[1040,256]{1,0:T(8,128)(2,1)S(1)} %fusion.1.refs_0_.refs_5_.refs_7_), channel_id=1, source_target_pairs={{0,96},{1,25},{8,104},{9,1},{16,112},{17,9},{24,120},{25,17},{32,0... | collective-permute-start | bytes 1597448 | tf_op jit(solution)/shard_map/ppermute | solution.py:55
  8.2 11.9 %collective-permute-start.1 = (bf16[1040,256]{1,0:T(8,128)(2,1)S(1)}, bf16[1040,256]{1,0:T(8,128)(2,1)S(1)}, u32[]{:S(2)}, u32[]{:S(2)}) collective-permute-start(bf16[1040,256]{1,0:T(8,128)(2,1)S(1)} %fusion.1.refs_0_.refs_5_.refs_7_), channel_id=1, source_target_pairs={{0,64},{1,17},{8,72},{9,25},{16,80},{17,1},{24,88},{25,9},{32,96},... | collective-permute-start | bytes 1597448 | tf_op jit(solution)/shard_map/ppermute | solution.py:55
  8.2 15.3 %collective-permute-start.2 = (bf16[1040,256]{1,0:T(8,128)(2,1)S(1)}, bf16[1040,256]{1,0:T(8,128)(2,1)S(1)}, u32[]{:S(2)}, u32[]{:S(2)}) collective-permute-start(bf16[1040,256]{1,0:T(8,128)(2,1)S(1)} %fusion.1.refs_0_.refs_5_.refs_7_), channel_id=1, source_target_pairs={{0,32},{1,9},{8,40},{9,17},{16,48},{17,25},{24,56},{25,1},{32,64},... | collective-permute-start | bytes 1597448 | tf_op jit(solution)/shard_map/ppermute | solution.py:55
  29.6 36.9 %collective-permute-start.3 = (bf16[8,256,256]{2,1,0:T(8,128)(2,1)}, bf16[8,256,256]{2,1,0:T(8,128)(2,1)}, u32[]{:S(2)}, u32[]{:S(2)}) collective-permute-start(bf16[8,256,256]{2,1,0:T(8,128)(2,1)} %get-tuple-element.41), channel_id=1, source_target_pairs={{0,24},{1,97},{8,0},{9,105},{16,8},{17,113},{24,16},{25,121},{32,5... | collective-permute-start | bytes 3145736 | tf_op jit(solution)/shard_map/ppermute | solution.py:55
  32.0 14.3 %collective-permute-start.6 = (bf16[1024,256]{1,0:T(8,128)(2,1)}, bf16[1024,256]{1,0:T(8,128)(2,1)}, u32[]{:S(2)}, u32[]{:S(2)}) collective-permute-start(bf16[1024,256]{1,0:T(8,128)(2,1)} %bitcast.14), channel_id=1, source_target_pairs={{0,96},{1,25},{8,104},{9,1},{16,112},{17,9},{24,120},{25,17},{32,0... | collective-permute-start | bytes 1572872 | tf_op jit(solution)/shard_map/ppermute | solution.py:55
  33.0 13.3 %collective-permute-start.7 = (bf16[1024,256]{1,0:T(8,128)(2,1)}, bf16[1024,256]{1,0:T(8,128)(2,1)}, u32[]{:S(2)}, u32[]{:S(2)}) collective-permute-start(bf16[1024,256]{1,0:T(8,128)(2,1)} %bitcast.15), channel_id=1, source_target_pairs={{0,64},{1,17},{8,72},{9,25},{16,80},{17,1},{24,88},{25,9},{32,96},... | collective-permute-start | bytes 1572872 | tf_op jit(solution)/shard_map/ppermute | solution.py:55
  33.0 27.4 %collective-permute-start.8 = (bf16[1024,256]{1,0:T(8,128)(2,1)}, bf16[1024,256]{1,0:T(8,128)(2,1)}, u32[]{:S(2)}, u32[]{:S(2)}) collective-permute-start(bf16[1024,256]{1,0:T(8,128)(2,1)} %bitcast.16), channel_id=1, source_target_pairs={{0,32},{1,9},{8,40},{9,17},{16,48},{17,25},{24,56},{25,1},{32,64},... | collective-permute-start | bytes 1572872 | tf_op jit(solution)/shard_map/ppermute | solution.py:55
  33.6 37.0 %collective-permute-start.4 = (bf16[8,256,256]{2,1,0:T(8,128)(2,1)}, bf16[8,256,256]{2,1,0:T(8,128)(2,1)}, u32[]{:S(2)}, u32[]{:S(2)}) collective-permute-start(bf16[8,256,256]{2,1,0:T(8,128)(2,1)} %get-tuple-element.42), channel_id=1, source_target_pairs={{0,16},{1,65},{8,24},{9,73},{16,0},{17,81},{24,8},{25,89},{32,48},... | collective-permute-start | bytes 3145736 | tf_op jit(solution)/shard_map/ppermute | solution.py:55
  46.3 25.2 %collective-permute-start.5 = (bf16[8,256,256]{2,1,0:T(8,128)(2,1)}, bf16[8,256,256]{2,1,0:T(8,128)(2,1)}, u32[]{:S(2)}, u32[]{:S(2)}) collective-permute-start(bf16[8,256,256]{2,1,0:T(8,128)(2,1)} %get-tuple-element.43), channel_id=1, source_target_pairs={{0,8},{1,33},{8,16},{9,41},{16,24},{17,49},{24,0},{25,57},{32,40},... | collective-permute-start | bytes 3145736 | tf_op jit(solution)/shard_map/ppermute | solution.py:55
  64.9 20.5 %collective-permute-start.9 = (bf16[8,256,256]{2,1,0:T(8,128)(2,1)}, bf16[8,256,256]{2,1,0:T(8,128)(2,1)}, u32[]{:S(2)}, u32[]{:S(2)}) collective-permute-start(bf16[8,256,256]{2,1,0:T(8,128)(2,1)} %get-tuple-element.45), channel_id=1, source_target_pairs={{0,24},{1,97},{8,0},{9,105},{16,8},{17,113},{24,16},{25,121},{32,5... | collective-permute-start | bytes 3145736 | tf_op jit(solution)/shard_map/ppermute | solution.py:55
  65.0 20.4 %collective-permute-start.10 = (bf16[8,256,256]{2,1,0:T(8,128)(2,1)}, bf16[8,256,256]{2,1,0:T(8,128)(2,1)}, u32[]{:S(2)}, u32[]{:S(2)}) collective-permute-start(bf16[8,256,256]{2,1,0:T(8,128)(2,1)} %get-tuple-element.46), channel_id=1, source_target_pairs={{0,16},{1,65},{8,24},{9,73},{16,0},{17,81},{24,8},{25,89},{32,48},... | collective-permute-start | bytes 3145736 | tf_op jit(solution)/shard_map/ppermute | solution.py:55
  66.6 27.7 %collective-permute-start.11 = (bf16[8,256,256]{2,1,0:T(8,128)(2,1)}, bf16[8,256,256]{2,1,0:T(8,128)(2,1)}, u32[]{:S(2)}, u32[]{:S(2)}) collective-permute-start(bf16[8,256,256]{2,1,0:T(8,128)(2,1)} %get-tuple-element.47), channel_id=1, source_target_pairs={{0,8},{1,33},{8,16},{9,41},{16,24},{17,49},{24,0},{25,57},{32,40},... | collective-permute-start | bytes 3145736 | tf_op jit(solution)/shard_map/ppermute | solution.py:55
  108.2 15.1 %collective-permute-start.12 = (bf16[1024,256]{1,0:T(8,128)(2,1)}, bf16[1024,256]{1,0:T(8,128)(2,1)}, u32[]{:S(2)}, u32[]{:S(2)}) collective-permute-start(bf16[1024,256]{1,0:T(8,128)(2,1)} %get-tuple-element.48.refs_0_.refs_5_.refs_7_), channel_id=1, source_target_pairs={{0,96},{1,25},{8,104},{9,1},{16,112},{17,9},{24,120},{25,17},{32,0... | collective-permute-start | bytes 1572872 | tf_op jit(solution)/shard_map/ppermute | solution.py:55
  111.2 12.1 %collective-permute-start.13 = (bf16[1024,256]{1,0:T(8,128)(2,1)}, bf16[1024,256]{1,0:T(8,128)(2,1)}, u32[]{:S(2)}, u32[]{:S(2)}) collective-permute-start(bf16[1024,256]{1,0:T(8,128)(2,1)} %get-tuple-element.48.refs_0_.refs_5_.refs_7_), channel_id=1, source_target_pairs={{0,64},{1,17},{8,72},{9,25},{16,80},{17,1},{24,88},{25,9},{32,96},... | collective-permute-start | bytes 1572872 | tf_op jit(solution)/shard_map/ppermute | solution.py:55
  111.2 15.5 %collective-permute-start.14 = (bf16[1024,256]{1,0:T(8,128)(2,1)}, bf16[1024,256]{1,0:T(8,128)(2,1)}, u32[]{:S(2)}, u32[]{:S(2)}) collective-permute-start(bf16[1024,256]{1,0:T(8,128)(2,1)} %get-tuple-element.48.refs_0_.refs_5_.refs_7_), channel_id=1, source_target_pairs={{0,32},{1,9},{8,40},{9,17},{16,48},{17,25},{24,56},{25,1},{32,64},... | collective-permute-start | bytes 1572872 | tf_op jit(solution)/shard_map/ppermute | solution.py:55
  131.2 27.3 %collective-permute-start.15 = (bf16[8,256,256]{2,1,0:T(8,128)(2,1)}, bf16[8,256,256]{2,1,0:T(8,128)(2,1)}, u32[]{:S(2)}, u32[]{:S(2)}) collective-permute-start(bf16[8,256,256]{2,1,0:T(8,128)(2,1)} %get-tuple-element.50), channel_id=1, source_target_pairs={{0,24},{1,97},{8,0},{9,105},{16,8},{17,113},{24,16},{25,121},{32,5... | collective-permute-start | bytes 3145736 | tf_op jit(solution)/shard_map/ppermute | solution.py:55
  131.3 8.4 %collective-permute-start.18 = (bf16[1024,256]{1,0:T(8,128)(2,1)}, bf16[1024,256]{1,0:T(8,128)(2,1)}, u32[]{:S(2)}, u32[]{:S(2)}) collective-permute-start(bf16[1024,256]{1,0:T(8,128)(2,1)} %get-tuple-element.49.refs_6_.refs_0_.refs_8_), channel_id=1, source_target_pairs={{0,96},{1,25},{8,104},{9,1},{16,112},{17,9},{24,120},{25,17},{32,0... | collective-permute-start | bytes 1572872 | tf_op jit(solution)/shard_map/ppermute | solution.py:55
  132.1 12.3 %collective-permute-start.19 = (bf16[1024,256]{1,0:T(8,128)(2,1)}, bf16[1024,256]{1,0:T(8,128)(2,1)}, u32[]{:S(2)}, u32[]{:S(2)}) collective-permute-start(bf16[1024,256]{1,0:T(8,128)(2,1)} %get-tuple-element.49.refs_6_.refs_0_.refs_8_), channel_id=1, source_target_pairs={{0,64},{1,17},{8,72},{9,25},{16,80},{17,1},{24,88},{25,9},{32,96},... | collective-permute-start | bytes 1572872 | tf_op jit(solution)/shard_map/ppermute | solution.py:55
  132.1 19.4 %collective-permute-start.20 = (bf16[1024,256]{1,0:T(8,128)(2,1)}, bf16[1024,256]{1,0:T(8,128)(2,1)}, u32[]{:S(2)}, u32[]{:S(2)}) collective-permute-start(bf16[1024,256]{1,0:T(8,128)(2,1)} %get-tuple-element.49.refs_6_.refs_0_.refs_8_), channel_id=1, source_target_pairs={{0,32},{1,9},{8,40},{9,17},{16,48},{17,25},{24,56},{25,1},{32,64},... | collective-permute-start | bytes 1572872 | tf_op jit(solution)/shard_map/ppermute | solution.py:55
  132.8 25.7 %collective-permute-start.16 = (bf16[8,256,256]{2,1,0:T(8,128)(2,1)}, bf16[8,256,256]{2,1,0:T(8,128)(2,1)}, u32[]{:S(2)}, u32[]{:S(2)}) collective-permute-start(bf16[8,256,256]{2,1,0:T(8,128)(2,1)} %get-tuple-element.51), channel_id=1, source_target_pairs={{0,16},{1,65},{8,24},{9,73},{16,0},{17,81},{24,8},{25,89},{32,48},... | collective-permute-start | bytes 3145736 | tf_op jit(solution)/shard_map/ppermute | solution.py:55
  139.7 31.1 %collective-permute-start.17 = (bf16[8,256,256]{2,1,0:T(8,128)(2,1)}, bf16[8,256,256]{2,1,0:T(8,128)(2,1)}, u32[]{:S(2)}, u32[]{:S(2)}) collective-permute-start(bf16[8,256,256]{2,1,0:T(8,128)(2,1)} %get-tuple-element.52), channel_id=1, source_target_pairs={{0,8},{1,33},{8,16},{9,41},{16,24},{17,49},{24,0},{25,57},{32,40},... | collective-permute-start | bytes 3145736 | tf_op jit(solution)/shard_map/ppermute | solution.py:55
  156.1 28.6 %collective-permute-start.21 = (bf16[8,256,256]{2,1,0:T(8,128)(2,1)}, bf16[8,256,256]{2,1,0:T(8,128)(2,1)}, u32[]{:S(2)}, u32[]{:S(2)}) collective-permute-start(bf16[8,256,256]{2,1,0:T(8,128)(2,1)} %get-tuple-element.54), channel_id=1, source_target_pairs={{0,24},{1,97},{8,0},{9,105},{16,8},{17,113},{24,16},{25,121},{32,5... | collective-permute-start | bytes 3145736 | tf_op jit(solution)/shard_map/ppermute | solution.py:55
  156.2 28.6 %collective-permute-start.22 = (bf16[8,256,256]{2,1,0:T(8,128)(2,1)}, bf16[8,256,256]{2,1,0:T(8,128)(2,1)}, u32[]{:S(2)}, u32[]{:S(2)}) collective-permute-start(bf16[8,256,256]{2,1,0:T(8,128)(2,1)} %get-tuple-element.55), channel_id=1, source_target_pairs={{0,16},{1,65},{8,24},{9,73},{16,0},{17,81},{24,8},{25,89},{32,48},... | collective-permute-start | bytes 3145736 | tf_op jit(solution)/shard_map/ppermute | solution.py:55
  158.5 35.0 %collective-permute-start.23 = (bf16[8,256,256]{2,1,0:T(8,128)(2,1)}, bf16[8,256,256]{2,1,0:T(8,128)(2,1)}, u32[]{:S(2)}, u32[]{:S(2)}) collective-permute-start(bf16[8,256,256]{2,1,0:T(8,128)(2,1)} %get-tuple-element.56), channel_id=1, source_target_pairs={{0,8},{1,33},{8,16},{9,41},{16,24},{17,49},{24,0},{25,57},{32,40},... | collective-permute-start | bytes 3145736 | tf_op jit(solution)/shard_map/ppermute | solution.py:55
  208.3 7.9 %collective-permute-start.24 = (f32[12,128]{1,0:T(8,128)S(1)}, f32[12,128]{1,0:T(8,128)S(1)}, u32[]{:S(2)}, u32[]{:S(2)}) collective-permute-start(f32[12,128]{1,0:T(8,128)S(1)} %add_add_fusion.2), channel_id=1, source_target_pairs={{0,1},{1,0},{2,3},{3,2},{4,5},{5,4},{6,7},{7,6},{8,9},{9,8},{10,11... | collective-permute-start | bytes 18440 | tf_op jit(solution)/shard_map/ppermute | solution.py:427
  216.2 4.4 %collective-permute-start.26 = (f32[12,128]{1,0:T(8,128)S(1)}, f32[12,128]{1,0:T(8,128)S(1)}, u32[]{:S(2)}, u32[]{:S(2)}) collective-permute-start(f32[12,128]{1,0:T(8,128)S(1)} %add.44), channel_id=1, source_target_pairs={{2,0},{4,2},{6,4},{0,6},{3,1},{5,3},{7,5},{1,7},{10,8},{12,10},{14... | collective-permute-start | bytes 18440 | tf_op jit(solution)/shard_map/ppermute | solution.py:42
  217.6 3.7 %collective-permute-start.27 = (f32[12,128]{1,0:T(8,128)S(1)}, f32[12,128]{1,0:T(8,128)S(1)}, u32[]{:S(2)}, u32[]{:S(2)}) collective-permute-start(f32[12,128]{1,0:T(8,128)S(1)} %add.44), channel_id=1, source_target_pairs={{6,0},{0,2},{2,4},{4,6},{7,1},{1,3},{3,5},{5,7},{14,8},{8,10},{10,... | collective-permute-start | bytes 18440 | tf_op jit(solution)/shard_map/ppermute | solution.py:42
  217.7 4.1 %collective-permute-start.25 = (f32[12,128]{1,0:T(8,128)S(1)}, f32[12,128]{1,0:T(8,128)S(1)}, u32[]{:S(2)}, u32[]{:S(2)}) collective-permute-start(f32[12,128]{1,0:T(8,128)S(1)} %add.44), channel_id=1, source_target_pairs={{4,0},{6,2},{0,4},{2,6},{5,1},{7,3},{1,5},{3,7},{12,8},{14,10},{8,... | collective-permute-start | bytes 18440 | tf_op jit(solution)/shard_map/ppermute | solution.py:42
  222.5 3.7 %collective-permute-start.30 = (f32[12,128]{1,0:T(8,128)S(1)}, f32[12,128]{1,0:T(8,128)S(1)}, u32[]{:S(2)}, u32[]{:S(2)}) collective-permute-start(f32[12,128]{1,0:T(8,128)S(1)} %add_add_fusion.1), channel_id=1, source_target_pairs={{24,0},{0,8},{8,16},{16,24},{25,1},{1,9},{9,17},{17,25},{26,2},{2,... | collective-permute-start | bytes 18440 | tf_op jit(solution)/shard_map/ppermute | solution.py:42
  223.3 4.0 %collective-permute-start.28 = (f32[12,128]{1,0:T(8,128)S(1)}, f32[12,128]{1,0:T(8,128)S(1)}, u32[]{:S(2)}, u32[]{:S(2)}) collective-permute-start(f32[12,128]{1,0:T(8,128)S(1)} %add_add_fusion.1), channel_id=1, source_target_pairs={{16,0},{24,8},{0,16},{8,24},{17,1},{25,9},{1,17},{9,25},{18,2},{26... | collective-permute-start | bytes 18440 | tf_op jit(solution)/shard_map/ppermute | solution.py:42
  227.3 7.4 %collective-permute-start.33 = (f32[12,128]{1,0:T(8,128)S(1)}, f32[12,128]{1,0:T(8,128)S(1)}, u32[]{:S(2)}, u32[]{:S(2)}) collective-permute-start(f32[12,128]{1,0:T(8,128)S(1)} %add_add_fusion), channel_id=1, source_target_pairs={{96,0},{0,32},{32,64},{64,96},{97,1},{1,33},{33,65},{65,97},{98,2}... | collective-permute-start | bytes 18440 | tf_op jit(solution)/shard_map/ppermute | solution.py:42
  232.8 4.0 %collective-permute-start.31 = (f32[12,128]{1,0:T(8,128)S(1)}, f32[12,128]{1,0:T(8,128)S(1)}, u32[]{:S(2)}, u32[]{:S(2)}) collective-permute-start(f32[12,128]{1,0:T(8,128)S(1)} %add_add_fusion), channel_id=1, source_target_pairs={{64,0},{96,32},{0,64},{32,96},{65,1},{97,33},{1,65},{33,97},{66,2}... | collective-permute-start | bytes 18440 | tf_op jit(solution)/shard_map/ppermute | solution.py:42
  (6 other events, 33.2 us)
